TPU v7x, 256 devices: a whole 4x4x8 slice. The times are simulated.
256 devices in a mesh: rep: 2 (over y_hi), fsdp: 128 (over z, x, y_lo, core).
Axes of the slice: x: 4, y: 4 (y_hi: 2, y_lo: 2; y = y_hi * 2 + y_lo), z: 8, core: 2. Of those that a mesh axis runs over, the one named last changes fastest.
Arguments:
- tokens: bfloat16 [131072, 4096], P(('rep', 'fsdp')), may hold values from -24 to 24
- value_cot: bfloat16 [131072, 1024], P(('rep', 'fsdp')), may hold values from -6 to 6
- value_weight: bfloat16 [2, 4096, 1024], P('rep', 'fsdp'), may hold values from -0.09375 to 0.09375
- global_params: float32 [16777216], P('fsdp'), may hold values from -6 to 6
- local_params: float32 [2, 16777216], P('rep', 'fsdp'), may hold values from -6 to 6
- momentum: float32 [16777216], P('fsdp'), may hold values from -3 to 3
Outputs:
- token_grad: bfloat16 [131072, 4096], P(('rep', 'fsdp'))
- value_grad: float32 [2, 4096, 1024], P('rep', 'fsdp')
- new_global: float32 [16777216], P('fsdp')
- new_moment: float32 [16777216], P('fsdp')
All inputs are finite; a program needn't handle non-finite values.
Results may differ from a plain program's by a relative error of at most 0.001.
Values may be sent and summed in bfloat16 or wider, within the bound.
No kernel may reach another device: no remote copies, remote signals or barrier semaphores. Data moves between devices by JAX's collectives and lax.ppermute only.
A program may use at most 128 MiB of HBM per device.

v0:
```python
import jax
import jax.numpy as jnp
from jax import lax
from jax.sharding import Mesh
from jax.sharding import PartitionSpec as P

FSDP = ("fsdp_0", "fsdp_1", "fsdp_2", "fsdp_3")
REP_FSDP = ("rep", "fsdp_0", "fsdp_1", "fsdp_2", "fsdp_3")


def split_up(x, dim, length):
    before, after = (x.shape[:dim], x.shape[dim + 1 :])
    return jnp.moveaxis(x.reshape(*before, length, -1, *after), dim, 0)


def summed_rows(x, chips, core, dim):
    sizes = (lax.axis_size(chips), lax.axis_size(core))
    tiles = split_up(x, dim, sizes[0] * sizes[1])
    inside = tiles.shape[1:]
    tiles = tiles.reshape(*sizes, *inside).swapaxes(0, 1).reshape(-1, *inside)
    tiles = lax.psum_scatter(tiles, core, scatter_dimension=0, tiled=True)
    return lax.psum_scatter(tiles, chips, scatter_dimension=0, tiled=True)[0]


def copy_for_each(x, axis):
    length = lax.axis_size(axis)
    return lax.all_to_all(jnp.broadcast_to(x[None], (length, *x.shape)), axis, 0, 0, tiled=True)


def over_copies(x, axis):
    everything = copy_for_each(x, axis)
    return jnp.sum(everything, axis=0)


def grad_term(tokens, columns):
    return lax.dot_general(
        tokens, columns, (((0,), (0,)), ((), ())), preferred_element_type=jnp.float32
    )


def shards(tokens, value_cot, value_weight, global_params, local_params, momentum):
    weight = value_weight[0]
    token_grad = lax.dot_general(
        value_cot,
        lax.all_gather(weight, FSDP, axis=0, tiled=True),
        (((1,), (1,)), ((), ())),
        preferred_element_type=jnp.float32,
    ).astype(jnp.bfloat16)
    groups = lax.axis_size(FSDP)
    factor = 1.0 / jnp.sqrt(jnp.float32(tokens.shape[0] * groups))
    summed = summed_rows(grad_term(tokens, value_cot), ("fsdp_0", "fsdp_1", "fsdp_2"), "fsdp_3", 0)
    value_grad = (summed * factor)[None]
    totals = over_copies(local_params[0], "rep")
    pseudo = global_params - totals / lax.axis_size("rep")
    new_moment = 0.9 * momentum + pseudo
    new_global = global_params - 0.7 * (pseudo + 0.9 * new_moment)
    return (token_grad, value_grad, new_global, new_moment)


def solution(mesh):
    split = Mesh(
        mesh.devices.reshape(mesh.shape["rep"], 8, 4, 2, 2),
        ("rep", "fsdp_0", "fsdp_1", "fsdp_2", "fsdp_3"),
    )
    return jax.shard_map(
        shards,
        mesh=split,
        in_specs=(
            P(REP_FSDP, None),
            P(REP_FSDP, None),
            P("rep", FSDP, None),
            P(FSDP),
            P("rep", FSDP),
            P(FSDP),
        ),
        out_specs=(P(REP_FSDP, None), P("rep", FSDP, None), P(FSDP), P(FSDP)),
        check_vma=False,
    )
```

profile of v0, /device:TPU:16, one launch (start us, length us, event | category | flops | bytes accessed | tf_op | source)
XLA Modules:
  0.0 405.7 jit_solution(8462821204067004481)
XLA Ops:
  8.0 0.0 copy-start
  8.0 0.0 reduce-scatter.3.cloned.1.call-start
  8.1 1.2 copy-done
  9.2 6.5 %fusion.5 = f32[4096,1024]{1,0:T(8,128)S(1)} fusion(bf16[512,4096]{1,0:T(8,128)(2,1)} %param.6, bf16[512,1024]{1,0:T(8,128)(2,1)S(1)} %copy-done), kind=kOutput, calls=%fused_computation.7 | convolution fusion | flops 4294967296 | bytes 22020096 | tf_op jit(solution)/shard_map/dot_general | solution.py:36
  15.7 6.1 %copy.12 = f32[2,64,32,1024]{3,2,1,0:T(8,128)} copy(f32[2,64,32,1024]{3,2,0,1:T(8,128)S(1)} %bitcast.14) | data formatting | bytes 33554432 | tf_op jit(solution)/shard_map/transpose | solution.py:20
  21.8 0.0 reduce-scatter.3.cloned.1.call-update
  21.8 0.0 copy-start.1
  21.8 0.0 copy-start.2
  21.8 0.0 all-gather.3.cloned.1.call-start
  21.9 0.5 all-gather.3.cloned.1.call-update
  22.4 0.0 reduce-scatter.5.cloned.1.call-start
  22.5 32.8 %reduce-scatter.3.cloned.1.call-done = f32[64,32,1024]{2,1,0:T(8,128)} async-done(((f32[128,32,1024]{2,1,0:T(8,128)}), f32[64,32,1024]{2,1,0:T(8,128)}) %reduce-scatter.3.cloned.1.call-update) | async-done | bytes 8388624 | tf_op jit(solution)/shard_map/reduce_scatter | solution.py:21
  55.3 0.0 reduce-scatter.5.cloned.1.call-update
  55.3 0.0 copy-done.1
  55.3 0.5 broadcast_in_dim.2
  55.9 19.6 %all_to_all.6 = f32[2,1,131072]{2,1,0:T(1,128)S(1)} all-to-all(f32[2,1,131072]{2,1,0:T(1,128)S(1)} %broadcast_in_dim.2), channel_id=1, replica_groups=mesh['rep'=2,'fsdp_0'=8,'fsdp_1'=4,'fsdp_2'=2,'fsdp_3'=2] {'rep'}, dimensions={0} | all-to-all | bytes 2097152 | tf_op jit(solution)/shard_map/all_to_all | solution.py:27
  75.4 1.5 reduce_sum.9
  76.9 0.0 copy-done.2
  76.9 2.1 multiply_subtract_fusion
  79.1 173.3 %all-gather.3.cloned.1.call-done = bf16[1,4096,1024]{2,1,0:T(8,128)(2,1)} async-done(((bf16[1,32,1024]{2,1,0:T(8,128)(2,1)}), bf16[1,4096,1024]{2,1,0:T(8,128)(2,1)}) %all-gather.3.cloned.1.call-update) | async-done | bytes 8388624 | tf_op jit(solution)/shard_map/all_gather | solution.py:45
  252.4 9.5 %fusion.2 = bf16[512,4096]{1,0:T(8,128)(2,1)} fusion(bf16[512,1024]{1,0:T(8,128)(2,1)S(1)} %copy-done, bf16[1,4096,1024]{2,1,0:T(8,128)(2,1)} %all-gather.3.cloned.1.call-done), kind=kOutput, calls=%fused_computation.2 | convolution fusion | flops 4297064448 | bytes 13631488 | tf_op jit(solution)/shard_map/dot_general | solution.py:43
  261.9 134.8 %reduce-scatter.5.cloned.1.call-done = f32[1,32,1024]{2,1,0:T(8,128)} async-done(((f32[64,32,1024]{2,1,0:T(8,128)}), f32[1,32,1024]{2,1,0:T(8,128)}) %reduce-scatter.5.cloned.1.call-update) | async-done | bytes 131088 | tf_op jit(solution)/shard_map/reduce_scatter | solution.py:22
  396.7 1.6 broadcast_multiply_fusion
Async XLA Ops:
  8.0 1.2 copy-start
  8.0 47.3 %reduce-scatter.3.cloned.1.call-start = ((), (), s32[]{:S(2)}) async-start(), calls=%async_computation.3 | async-start | bytes 25165824 | tf_op jit(solution)/shard_map/reduce_scatter | solution.py:21
  21.8 33.5 %copy-start.1 = (f32[1,131072]{1,0:T(1,128)S(1)}, f32[1,131072]{1,0:T(1,128)}, u32[]{:S(2)}) copy-start(f32[1,131072]{1,0:T(1,128)} %param.10) | copy-start | bytes 1572868
  21.8 55.1 %copy-start.2 = (f32[131072]{0:T(1024)S(1)}, f32[131072]{0:T(1024)}, u32[]{:S(2)}) copy-start(f32[131072]{0:T(1024)} %param.9) | copy-start | bytes 1572868
  21.8 230.5 %all-gather.3.cloned.1.call-start = ((), (), s32[]{:S(2)}) async-start(), calls=%async_computation.5 | async-start | bytes 8454144 | tf_op jit(solution)/shard_map/all_gather | solution.py:45
  22.4 374.3 %reduce-scatter.5.cloned.1.call-start = ((), (), s32[]{:S(2)}) async-start(), calls=%async_computation.4 | async-start | bytes 8519680 | tf_op jit(solution)/shard_map/reduce_scatter | solution.py:22
Sparse Core Ops, SparseCore 0:
  21.9 33.3 reduce-scatter.2
  57.8 338.8 reduce-scatter.4
Sparse Core Ops, SparseCore 1:
  24.2 228.1 all-gather.2
where the time goes:
time: 406 us
  waiting for transfers between devices  341 us (84%)
  blocking collectives  19.6 us (5%)
  matrix products  16 us (4%)
  between operations  15.5 us (4%)
  local copies, waits for them, and re-layouts  7.79 us (2%)
  other arithmetic  5.2 us (1%)
    all_gather x1, waiting for transfers between devices, shards(): lax.all_gather(weight, FSDP, axis=0, tiled=True)  173 us
    reduce_scatter x1, waiting for transfers between devices, summed_rows(): return lax.psum_scatter(tiles, chips, scatter_dimension=0, tiled=True)[0]  135 us
    reduce_scatter x1, waiting for transfers between devices, summed_rows(): tiles = lax.psum_scatter(tiles, core, scatter_dimension=0, tiled=True)  32.8 us
    all_to_all x1, blocking collectives, copy_for_each(): lax.all_to_all(jnp.broadcast_to(x[None], (length, *x.shape)), axis, 0, 0,...  19.6 us
    dot_general x1, matrix products, shards(): lax.dot_general(value_cot, lax.all_gather(weight, FSDP, axis=0, tiled=Tru...  9.49 us
  transfers between devices with their start and end apart: 3, of which 3 were waited for; matrix products, arithmetic and copies ran while one was open for 3% of the time, Pallas kernels for 0%

commit v1 on v0

--- a/solution.py
+++ b/solution.py
@@ -40,9 +40,15 @@
 
 def shards(tokens, value_cot, value_weight, global_params, local_params, momentum):
     weight = value_weight[0]
+
+    def wall_compute(base_x):
+        a_now = jnp.stack(lax.axis_size(FSDP) * [base_x], axis=0)
+        side_arr = lax.all_to_all(a_now, FSDP, 0, 0)
+        return jnp.concatenate(side_arr, axis=0)
+
     token_grad = lax.dot_general(
         value_cot,
-        lax.all_gather(weight, FSDP, axis=0, tiled=True),
+        wall_compute(weight),
         (((1,), (1,)), ((), ())),
         preferred_element_type=jnp.float32,
     ).astype(jnp.bfloat16)

time: 406 us -> 478 us (1.18)
  waiting for transfers between devices: 341 us -> 394 us
  starting transfers between devices: 0.12 us -> 14.5 us
  local copies, waits for them, and re-layouts: 7.79 us -> 15.3 us
    all_to_all x0 -> x1, waiting for transfers between devices: none -> 223 us  [wall_compute(): side_arr = lax.all_to_all(a_now, FSDP, 0, 0)]
    all_gather x1 -> x0, waiting for transfers between devices: 173 us -> none  [shards(): lax.all_gather(weight, FSDP, axis=0, tiled=True)]
    reduce_scatter x1, waiting for transfers between devices: 135 us -> 171 us  [summed_rows(): return lax.psum_scatter(tiles, chips, scatter_dimension=0, tiled=True)[0]]
    reduce_scatter x1, waiting for transfers between devices: 32.8 us -> 0.02 us  [summed_rows(): tiles = lax.psum_scatter(tiles, core, scatter_dimension=0, tiled=True)]
    all_to_all x0 -> x1, starting transfers between devices: none -> 14.4 us  [wall_compute(): side_arr = lax.all_to_all(a_now, FSDP, 0, 0)]
    another operation x0 -> x1, local copies, waits for them, and re-layouts: none -> 6.46 us  [wall_compute(): a_now = jnp.stack(lax.axis_size(FSDP) * [base_x], axis=0)]
  transfers between devices with their start and end apart: 3 -> 3, of which waited for: 3 -> 2; matrix products, arithmetic and copies ran while one was open for 3% -> 4% of each run, Pallas kernels for 0% -> 0%
where the time goes in v1:
time: 478 us; the launch traced here: 475 us
  waiting for transfers between devices  394 us (82%)
  blocking collectives  16.4 us (3%)
  matrix products  16 us (3%)
  local copies, waits for them, and re-layouts  15.3 us (3%)
  starting transfers between devices  14.5 us (3%)
  between operations  14.1 us (3%)
  other arithmetic  5.2 us (1%)
    all_to_all x1, waiting for transfers between devices, wall_compute(): side_arr = lax.all_to_all(a_now, FSDP, 0, 0)  223 us
    reduce_scatter x1, waiting for transfers between devices, summed_rows(): return lax.psum_scatter(tiles, chips, scatter_dimension=0, tiled=True)[0]  171 us
    all_to_all x1, blocking collectives, copy_for_each(): lax.all_to_all(jnp.broadcast_to(x[None], (length, *x.shape)), axis, 0, 0,...  16.4 us
    all_to_all x1, starting transfers between devices, wall_compute(): side_arr = lax.all_to_all(a_now, FSDP, 0, 0)  14.4 us
  transfers between devices with their start and end apart: 3, of which 2 were waited for; matrix products, arithmetic and copies ran while one was open for 4% of the time, Pallas kernels for 0%

profile of v1, /device:TPU:16, one launch (start us, length us, event | category | flops | bytes accessed | tf_op | source)
XLA Modules:
  0.0 475.3 jit_solution(15904543256004525923)
XLA Ops:
  7.2 0.0 copy-start
  7.2 0.0 reduce-scatter.3.cloned.1.call-start
  7.2 1.2 copy-done
  8.4 6.5 %fusion = f32[4096,1024]{1,0:T(8,128)S(1)} fusion(bf16[512,4096]{1,0:T(8,128)(2,1)} %param.6, bf16[512,1024]{1,0:T(8,128)(2,1)S(1)} %copy-done), kind=kOutput, calls=%fused_computation.5 | convolution fusion | flops 4294967296 | bytes 22020096 | tf_op jit(solution)/shard_map/dot_general | solution.py:36
  14.9 6.1 %copy.12 = f32[2,64,32,1024]{3,2,1,0:T(8,128)} copy(f32[2,64,32,1024]{3,2,0,1:T(8,128)S(1)} %bitcast.12) | data formatting | bytes 33554432 | tf_op jit(solution)/shard_map/transpose | solution.py:20
  21.0 0.0 copy-start.1
  21.0 0.0 reduce-scatter.3.cloned.1.call-update
  21.0 1.0 copy-done.1
  22.0 0.5 broadcast_in_dim.2
  22.5 16.4 %all_to_all.11 = f32[2,1,131072]{2,1,0:T(1,128)S(1)} all-to-all(f32[2,1,131072]{2,1,0:T(1,128)S(1)} %broadcast_in_dim.2), channel_id=1, replica_groups=mesh['rep'=2,'fsdp_0'=8,'fsdp_1'=4,'fsdp_2'=2,'fsdp_3'=2] {'rep'}, dimensions={0} | all-to-all | bytes 2097152 | tf_op jit(solution)/shard_map/all_to_all | solution.py:27
  39.0 0.0 copy-done.3
  39.0 6.5 %stack.3 = bf16[128,32,1024]{2,1,0:T(8,128)(2,1)} broadcast(bf16[32,1024]{1,0:T(8,128)(2,1)S(1)} %bitcast.14), dimensions={1,2} | broadcast | bytes 8454144 | tf_op jit(solution)/shard_map/stack | solution.py:45
  45.4 14.4 %all-to-all-start = ((bf16[128,32,1024]{2,1,0:T(8,128)(2,1)}), bf16[128,32,1024]{2,1,0:T(8,128)(2,1)}, u32[]{:S(2)}, u32[]{:S(2)}) async-start(bf16[128,32,1024]{2,1,0:T(8,128)(2,1)} %stack.3), calls=%async_computation | async-start | bytes 16777216 | tf_op jit(solution)/shard_map/all_to_all | solution.py:46
  59.9 0.0 copy-start.2
  59.9 0.0 reduce-scatter.5.cloned.1.call-start
  59.9 0.0 reduce-scatter.3.cloned.1.call-done
  59.9 0.7 reduce-scatter.5.cloned.1.call-update
  60.6 1.5 reduce_sum.9
  62.1 0.0 copy-done.2
  62.1 2.1 multiply_subtract_fusion
  64.3 222.6 %all-to-all-done = bf16[128,32,1024]{2,1,0:T(8,128)(2,1)} async-done(((bf16[128,32,1024]{2,1,0:T(8,128)(2,1)}), bf16[128,32,1024]{2,1,0:T(8,128)(2,1)}, u32[]{:S(2)}, u32[]{:S(2)}) %all-to-all-start) | async-done | bytes 8388640 | tf_op jit(solution)/shard_map/all_to_all | solution.py:46
  286.9 9.5 %convolution_convert_fusion = bf16[512,4096]{1,0:T(8,128)(2,1)} fusion(bf16[512,1024]{1,0:T(8,128)(2,1)S(1)} %copy-done, bf16[4096,1024]{1,0:T(8,128)(2,1)} %bitcast.1), kind=kOutput, calls=%fused_computation | convolution fusion | flops 4297064448 | bytes 13631488 | tf_op jit(solution)/shard_map/dot_general | solution.py:49
  296.3 170.5 %reduce-scatter.5.cloned.1.call-done = f32[1,32,1024]{2,1,0:T(8,128)} async-done(((f32[64,32,1024]{2,1,0:T(8,128)}), f32[1,32,1024]{2,1,0:T(8,128)}) %reduce-scatter.5.cloned.1.call-update) | async-done | bytes 131088 | tf_op jit(solution)/shard_map/reduce_scatter | solution.py:22
  466.9 1.6 broadcast_multiply_fusion
  (1 shorter events, 0.0 us)
Async XLA Ops:
  7.2 1.2 copy-start
  7.2 52.8 %reduce-scatter.3.cloned.1.call-start = ((), (), s32[]{:S(2)}) async-start(), calls=%async_computation.4 | async-start | bytes 25165824 | tf_op jit(solution)/shard_map/reduce_scatter | solution.py:21
  21.0 1.0 copy-start.1
  21.0 18.0 %copy-start.3 = (bf16[1,32,1024]{2,1,0:T(8,128)(2,1)S(1)}, bf16[1,32,1024]{2,1,0:T(8,128)(2,1)}, u32[]{:S(2)}) copy-start(bf16[1,32,1024]{2,1,0:T(8,128)(2,1)} %param.8) | copy-start | bytes 196612
  45.4 241.4 %all-to-all-start = ((bf16[128,32,1024]{2,1,0:T(8,128)(2,1)}), bf16[128,32,1024]{2,1,0:T(8,128)(2,1)}, u32[]{:S(2)}, u32[]{:S(2)}) async-start(bf16[128,32,1024]{2,1,0:T(8,128)(2,1)} %stack.3), calls=%async_computation | async-start | bytes 16777216 | tf_op jit(solution)/shard_map/all_to_all | solution.py:46
  59.9 2.3 copy-start.2
  59.9 407.0 %reduce-scatter.5.cloned.1.call-start = ((), (), s32[]{:S(2)}) async-start(), calls=%async_computation.5 | async-start | bytes 8519680 | tf_op jit(solution)/shard_map/reduce_scatter | solution.py:22
Sparse Core Ops, SparseCore 0:
  21.1 33.3 reduce-scatter.2
  63.2 403.6 reduce-scatter.4
